TPU v7x, 8 devices: a whole 2x2x1 slice. The times are simulated.
8 devices in a mesh: rep: 1 (over z), head: 2 (over y), seq: 4 (over x, core).
Axes of the slice: x: 2, y: 2, z: 1, core: 2. Of those that a mesh axis runs over, the one named last changes fastest.
Arguments:
- tokens: bfloat16 [64, 4096], P('rep')
- w_query: bfloat16 [4096, 4096], replicated
- w_key: bfloat16 [4096, 1024], replicated
- w_value: bfloat16 [4096, 1024], replicated
- w_out: bfloat16 [4096, 4096], P(('head', 'seq'))
- k_cache: bfloat16 [64, 1024, 8, 128], P('rep', 'seq', 'head')
- v_cache: bfloat16 [64, 1024, 8, 128], P('rep', 'seq', 'head')
- positions: int32 [64], P('rep')
Outputs:
- output 1: bfloat16 [64, 4096], P('rep')
- output 2: bfloat16 [64, 1024, 8, 128], P('rep', 'seq', 'head')
- output 3: bfloat16 [64, 1024, 8, 128], P('rep', 'seq', 'head')
All inputs are finite; a program needn't handle non-finite values.
Results may differ from a plain program's by a relative error of at most 0.00655092.
Values are sent between devices in bfloat16 or wider.
A program may use at most 1 GiB of HBM per device.

v0:
```python
import jax
import jax.numpy as jnp
from jax import lax
from jax.sharding import PartitionSpec as P


def solution(mesh):
    head_devs = mesh.shape['head']
    cache_spec = P('rep', 'seq', 'head', None)

    def local_step(tokens, w_query, w_key, w_value, w_out, k_cache, v_cache, positions):
        batch_size, shard_len, kv_local, head_dim = k_cache.shape
        heads_total = w_query.shape[1] // head_dim
        groups = heads_total // (kv_local * head_devs)
        q_cols = kv_local * groups * head_dim
        kv_cols = kv_local * head_dim
        wo_rows = w_out.shape[0]
        head_idx = lax.axis_index('head')
        seq_idx = lax.axis_index('seq')
        wq_local = lax.dynamic_slice_in_dim(w_query, head_idx * q_cols, q_cols, axis=1)
        wk_local = lax.dynamic_slice_in_dim(w_key, head_idx * kv_cols, kv_cols, axis=1)
        wv_local = lax.dynamic_slice_in_dim(w_value, head_idx * kv_cols, kv_cols, axis=1)
        query = jnp.dot(tokens, wq_local, preferred_element_type=jnp.float32).astype(jnp.bfloat16).reshape(batch_size, kv_local, groups, head_dim)
        new_key = jnp.dot(tokens, wk_local, preferred_element_type=jnp.float32).astype(jnp.bfloat16).reshape(batch_size, 1, kv_local, head_dim)
        new_value = jnp.dot(tokens, wv_local, preferred_element_type=jnp.float32).astype(jnp.bfloat16).reshape(batch_size, 1, kv_local, head_dim)
        slot_ids = seq_idx * shard_len + jnp.arange(shard_len, dtype=jnp.int32)
        is_slot = (slot_ids[None, :] == positions[:, None])[:, :, None, None]
        k_new = jnp.where(is_slot, new_key, k_cache)
        v_new = jnp.where(is_slot, new_value, v_cache)
        scores = jnp.einsum('bkgd,btkd->bkgt', query, k_new, preferred_element_type=jnp.float32) * head_dim ** -0.5
        valid_mask = (slot_ids[None, :] <= positions[:, None])[:, None, None, :]
        scores = jnp.where(valid_mask, scores, -jnp.inf)
        local_max = jnp.max(scores, axis=-1)
        safe_max = jnp.where(jnp.isfinite(local_max), local_max, 0.0)
        weights = jnp.exp(scores - safe_max[..., None])
        local_sum = jnp.sum(weights, axis=-1)
        local_mix = jnp.einsum('bkgt,btkd->bkgd', weights.astype(jnp.bfloat16), v_new, preferred_element_type=jnp.float32)
        global_max = lax.pmax(local_max, 'seq')
        rescale = jnp.exp(local_max - global_max)
        total_sum, total_mix = lax.psum((local_sum * rescale, local_mix * rescale[..., None]), 'seq')
        attn_flat = (total_mix / total_sum[..., None]).astype(jnp.bfloat16).reshape(batch_size, q_cols)
        attn_part = lax.dynamic_slice_in_dim(attn_flat, seq_idx * wo_rows, wo_rows, axis=1)
        y_part = jnp.dot(attn_part, w_out, preferred_element_type=jnp.float32)
        y_total = lax.psum(y_part, ('head', 'seq'))
        return y_total.astype(jnp.bfloat16), k_new, v_new

    return jax.shard_map(
        local_step,
        mesh=mesh,
        in_specs=(P('rep', None), P(), P(), P(), P(('head', 'seq'), None), cache_spec, cache_spec, P('rep')),
        out_specs=(P('rep', None), cache_spec, cache_spec),
        check_vma=False,
    )
```

profile of v0, /device:TPU:0, one launch (start us, length us, event | category | flops | bytes accessed | tf_op | source)
XLA Modules:
  0.0 157.6 jit_solution(2677683790038055645)
XLA Ops:
  7.2 0.0 copy-start
  7.2 0.0 copy-start.2
  7.2 0.0 all-reduce.3.cloned.1.call-start
  7.3 1.0 copy-done
  8.2 3.0 %fusion.31 = bf16[64,512]{1,0:T(8,128)(2,1)S(1)} fusion(bf16[64,4096]{1,0:T(8,128)(2,1)S(1)} %copy-done, bf16[4096,1024]{1,0:T(8,128)(2,1)} %param.10, s32[]{:T(128)S(6)} %select_n.30), kind=kOutput, calls=%fused_computation.19 | convolution fusion | flops 268468224 | bytes 4784132 | tf_op jit(solution)/shard_map/dot_general | solution.py:24
  11.3 3.0 %fusion.28 = bf16[64,512]{1,0:T(8,128)(2,1)S(1)} fusion(bf16[64,4096]{1,0:T(8,128)(2,1)S(1)} %copy-done, bf16[4096,1024]{1,0:T(8,128)(2,1)} %param.11, s32[]{:T(128)S(6)} %select_n.30), kind=kOutput, calls=%fused_computation.18 | convolution fusion | flops 268468224 | bytes 4784132 | tf_op jit(solution)/shard_map/dot_general | solution.py:25
  14.3 8.8 %fusion.13 = bf16[64,2048]{1,0:T(8,128)(2,1)S(1)} fusion(bf16[64,4096]{1,0:T(8,128)(2,1)S(1)} %copy-done, bf16[4096,4096]{1,0:T(8,128)(2,1)} %param.9, s32[]{:T(128)S(6)} %select_n.29), kind=kOutput, calls=%fused_computation.13 | convolution fusion | flops 1073872896 | bytes 17563652 | tf_op jit(solution)/shard_map/dot_general | solution.py:23
  23.1 0.2 reshape.75
  23.3 0.0 copy-done.2
  23.3 0.1 broadcast_compare_fusion.1
  23.4 25.9 %broadcast_select_fusion.1 = (bf16[64,256,4,128]{3,2,1,0:T(4,128)(2,1)}, bf16[64,256,4,128]{3,2,1,0:T(4,128)(2,1)}) fusion(bf16[64,256,4,128]{3,2,1,0:T(4,128)(2,1)} %param.13, pred[64,256]{1,0:T(8,128)(4,1)S(1)} %get-tuple-element.8, bf16[64,4,128]{2,1,0:T(4,128)(2,1)S(1)} %broadcast_in_dim.55, bf16[64,256,4,128]{3,2,1,0:T(4,128)(2,1)} %param.14, ...), kind=kLoop, calls=%fused_computation.7 | loop fusion | flops 16777216 | bytes 67256320 | tf_op jit(solution)/shard_map/jit(_where)/select_n | solution.py:28
  49.3 0.0 copy-start.1
  49.3 10.4 %fusion.48 = (f32[64,4,4]{2,1,0:T(4,128)S(1)}, f32[64,4,4,256]{3,2,1,0:T(4,128)S(1)}) fusion(bf16[64,4,4,128]{3,2,1,0:T(4,128)(2,1)S(1)} %reshape.75, bf16[64,256,4,128]{3,2,1,0:T(4,128)(2,1)} %get-tuple-element.5, pred[64,256]{1,0:T(8,128)(4,1)S(1)} %get-tuple-element.7), kind=kOutput, calls=%fused_computation.38 | convolution fusion | flops 67894272 | bytes 18108416 | tf_op jit(solution)/shard_map/bkgd,btkd->bkgt/dot_general | solution.py:30
  59.8 14.8 %pmax.7 = f32[64,4,4]{2,1,0:T(4,128)S(1)} all-reduce(f32[64,4,4]{2,1,0:T(4,128)S(1)} %get-tuple-element.9), channel_id=1, replica_groups=mesh['rep'=1,'head'=2,'seq'=4] {'seq'}, use_global_device_ids=true, to_apply=%region_1.2 | all-reduce | flops 1024 | bytes 8192 | tf_op jit(solution)/shard_map/pmax | solution.py:38
  74.6 0.8 fusion.37
  75.4 8.8 %fusion.19 = f32[64,4,4,128]{3,2,1,0:T(4,128)} fusion(bf16[64,256,4,128]{3,2,1,0:T(4,128)(2,1)} %get-tuple-element.6, f32[64,4,4,256]{3,2,1,0:T(4,128)S(1)} %get-tuple-element.10, f32[64,4,4]{2,1,0:T(4,128)S(1)} %is-finite_select_fusion, f32[64,4,4]{2,1,0:T(4,128)S(1)} %bitcast.20), kind=kOutput, calls=%fused_computation.15 | convolution fusion | flops 67764224 | bytes 18358272 | tf_op jit(solution)/shard_map/bkgt,btkd->bkgd/dot_general | solution.py:37
  84.2 0.0 all-reduce.3.cloned.1.call-update
  84.3 13.9 %psum.22 = f32[64,4,4]{2,1,0:T(4,128)S(1)} all-reduce(f32[64,4,4]{2,1,0:T(4,128)S(1)} %bitcast.18), channel_id=1, replica_groups=mesh['rep'=1,'head'=2,'seq'=4] {'seq'}, use_global_device_ids=true, to_apply=%region_4.5 | all-reduce | flops 1024 | bytes 8192 | tf_op jit(solution)/shard_map/psum | solution.py:40
  98.2 14.9 %all-reduce.3.cloned.1.call-done = f32[64,4,4,128]{3,2,1,0:T(4,128)} async-done(((f32[64,4,4,128]{3,2,1,0:T(4,128)}), f32[64,4,4,128]{3,2,1,0:T(4,128)}) %all-reduce.3.cloned.1.call-update) | async-done | bytes 524304 | tf_op jit(solution)/shard_map/psum | solution.py:40
  113.0 1.4 divide_convert_fusion
  114.4 0.2 reshape.76
  114.6 3.0 %fusion.41 = f32[64,4096]{1,0:T(8,128)S(1)} fusion(bf16[512,4096]{1,0:T(8,128)(2,1)} %param.12, bf16[64,2048]{1,0:T(8,128)(2,1)S(1)} %reshape.76, s32[]{:T(128)S(6)} %select_n.35), kind=kOutput, calls=%fused_computation.28 | convolution fusion | flops 268435456 | bytes 5308420 | tf_op jit(solution)/shard_map/dot_general | solution.py:43
  117.7 33.1 %all-reduce.4 = bf16[64,4096]{1,0:T(8,128)(2,1)} all-reduce(f32[64,4096]{1,0:T(8,128)S(1)} %fusion.41), channel_id=1, replica_groups=mesh['rep'=1,'head'=2,'seq'=4] {'head','seq'}, use_global_device_ids=true, to_apply=%region_5.6 | all-reduce | flops 262144 | bytes 1572864 | tf_op jit(solution)/shard_map/psum | solution.py:44
  150.7 0.0 copy-done.1
  (5 shorter events, 0.1 us)
Async XLA Ops:
  7.2 1.1 copy-start
  7.2 16.1 %copy-start.2 = (s32[64]{0:T(128)S(1)}, s32[64]{0:T(128)}, u32[]{:S(2)}) copy-start(s32[64]{0:T(128)} %param.15) | copy-start | bytes 772
  7.2 105.8 %all-reduce.3.cloned.1.call-start = ((), (), s32[]{:S(2)}) async-start(), calls=%async_computation | async-start | bytes 1048576 | tf_op jit(solution)/shard_map/psum | solution.py:40
  49.3 101.4 %copy-start.1 = (bf16[64,4096]{1,0:T(8,128)(2,1)S(1)}, bf16[64,4096]{1,0:T(8,128)(2,1)}, u32[]{:S(2)}) copy-start(bf16[64,4096]{1,0:T(8,128)(2,1)} %param.8) | copy-start | bytes 1572868
Sparse Core Ops, SparseCore 0:
  84.4 28.6 all-reduce.2
where the time goes:
time: 158 us
  blocking collectives  61.8 us (39%)
  matrix products  37 us (23%)
  other arithmetic  28.3 us (18%)
  waiting for transfers between devices  14.9 us (9%)
  between operations  14.2 us (9%)
    psum x1, blocking collectives, local_step(): y_total = lax.psum(y_part, ('head', 'seq'))  33.1 us
    select_n x1, other arithmetic, local_step(): k_new = jnp.where(is_slot, new_key, k_cache)  25.9 us
    psum x1, waiting for transfers between devices, local_step(): lax.psum((local_sum * rescale, local_mix * rescale[..., None]), 'seq')  14.9 us
    pmax x1, blocking collectives, local_step(): global_max = lax.pmax(local_max, 'seq')  14.8 us
    psum x1, blocking collectives, local_step(): lax.psum((local_sum * rescale, local_mix * rescale[..., None]), 'seq')  13.9 us
    dot_general x1, matrix products, local_step(): jnp.einsum('bkgd,btkd->bkgt', query, k_new, preferred_element_type=jnp.fl...  10.4 us
    dot_general x1, matrix products, local_step(): jnp.dot(tokens, wq_local, preferred_element_type=jnp.float32)  8.8 us
    dot_general x1, matrix products, local_step(): jnp.einsum('bkgt,btkd->bkgd', weights.astype(jnp.bfloat16), v_new, prefer...  8.79 us
  transfers between devices with their start and end apart: 1, of which 1 were waited for; matrix products, arithmetic and copies ran while one was open for 0% of the time, Pallas kernels for 0%

commit v1 on v0

v1 whole, which is shorter than its diff:
```python
import functools

import jax
import jax.numpy as jnp
from jax import lax
from jax.experimental import pallas as pl
from jax.experimental.pallas import tpu as pltpu
from jax.sharding import PartitionSpec as P

MESH = pl.DeviceIdType.MESH
BF16 = jnp.bfloat16
F32 = jnp.float32
MIB = 2 ** 20
GB = 8
D = 128
LOG2E = 1.4426950408889634


def attend_kernel(dims, pos_ref, x_ref, wq, wk, wv, kc, vc, ko, vo, mix_ref, st_ref,
                  k_vm, v_vm, w_vm, q_s, nk_s, nv_s, s_s, w_sem, k_sem, v_sem, ko_sem, vo_sem):
    kv, groups, shard, n_groups, slots = dims
    heads = kv * groups
    rows = shard * kv
    lanes = heads * GB
    head_i, seq_i = lax.axis_index("head"), lax.axis_index("seq")
    base = seq_i * shard
    cols = kv * D
    n_q = heads // kv

    def w_copy(c):
        if c < n_q:
            src, at = wq, head_i * (heads * D) + c * cols
        else:
            src, at = (wk, wv)[c - n_q], head_i * cols
        at = pl.multiple_of(at, cols)
        return pltpu.make_async_copy(src.at[:, pl.ds(at, cols)], w_vm.at[c % slots], w_sem.at[c % slots])

    def k_copy(g):
        at = pl.ds(g * GB, GB)
        return pltpu.make_async_copy(kc.at[at], k_vm.at[at], k_sem.at[g])

    def v_copy(g):
        at = pl.ds(g * GB, GB)
        return pltpu.make_async_copy(vc.at[at], v_vm.at[at], v_sem.at[g])

    def ko_copy(g):
        at = pl.ds(g * GB, GB)
        return pltpu.make_async_copy(k_vm.at[at], ko.at[at], ko_sem.at[g])

    def vo_copy(g):
        at = pl.ds(g * GB, GB)
        return pltpu.make_async_copy(v_vm.at[at], vo.at[at], vo_sem.at[g])

    n_w = n_q + 2
    ahead = 4
    for c in range(min(slots, n_w)):
        w_copy(c).start()
    issued = 0
    for c in range(n_w):
        w_copy(c).wait()
        r = jnp.dot(x_ref[...], w_vm[c % slots], preferred_element_type=F32)
        r = r.astype(BF16).astype(F32)
        for i in range(kv):
            part = r[:, i * D:(i + 1) * D]
            if c < n_q:
                q_s[c * kv + i] = part
            elif c == n_q:
                nk_s[i] = part
            else:
                nv_s[i] = part
        if c + slots < n_w:
            w_copy(c + slots).start()
        else:
            while issued < min(ahead, n_groups) and issued <= (c + slots - n_w + 1):
                k_copy(issued).start()
                v_copy(issued).start()
                issued += 1
    for g in range(issued, min(ahead, n_groups)):
        k_copy(g).start()
        v_copy(g).start()

    r16 = lax.broadcasted_iota(jnp.int32, (16, D), 0)

    def new_rows(src, b):
        out = jnp.broadcast_to(src[kv - 1, pl.ds(b, 1), :], (16, D))
        for j in range(kv - 1):
            out = jnp.where(r16 % kv == j, jnp.broadcast_to(src[j, pl.ds(b, 1), :], (16, D)), out)
        return out

    sub = lax.broadcasted_iota(jnp.int32, (8, lanes), 0)
    lane = lax.broadcasted_iota(jnp.int32, (8, lanes), 1)
    lane_d = lax.broadcasted_iota(jnp.int32, (D, lanes), 1)
    row_l = lax.broadcasted_iota(jnp.int32, (lanes, D), 0)
    per_tile = 8 // kv
    scale2 = (D ** -0.5) * LOG2E

    def group(g, carry):
        @pl.when(g + ahead < n_groups)
        def _():
            k_copy(g + ahead).start()
            v_copy(g + ahead).start()
        k_copy(g).wait()
        v_copy(g).wait()
        pos_row = jnp.zeros((8, lanes), jnp.int32)
        for i in range(GB):
            b = g * GB + i
            t = pos_ref[b] - base
            pos_row = jnp.where(lane % GB == i, t, pos_row)

            @pl.when(jnp.logical_and(t >= 0, t < shard))
            def _():
                at = pl.ds(pl.multiple_of((t // (16 // kv)) * 16, 16), 16)
                hit = r16 // kv == t % (16 // kv)
                k_vm[b, at, :] = jnp.where(hit, new_rows(nk_s, b), k_vm[b, at, :].astype(F32)).astype(BF16)
                v_vm[b, at, :] = jnp.where(hit, new_rows(nv_s, b), v_vm[b, at, :].astype(F32)).astype(BF16)
        ko_copy(g).start()
        vo_copy(g).start()

        q_t = q_s[:, pl.ds(pl.multiple_of(g * GB, GB), GB), :].reshape(lanes, D).T
        acc = None
        for p in range(GB // 2):
            keys = jnp.concatenate([k_vm[g * GB + 2 * p], k_vm[g * GB + 2 * p + 1]], axis=1)
            qs = jnp.concatenate([jnp.where(lane_d % GB == 2 * p, q_t, 0.0),
                                  jnp.where(lane_d % GB == 2 * p + 1, q_t, 0.0)], axis=0).astype(BF16)
            s = jnp.dot(keys, qs, preferred_element_type=F32)
            acc = s if acc is None else acc + s
        limit = jnp.where(sub % kv == lane // (groups * GB), pos_row - sub // kv, -1)
        tile_t = lax.broadcasted_iota(jnp.int32, (rows // 8, 8, lanes), 0) * per_tile
        s3 = jnp.where(limit[None] >= tile_t, acc.reshape(rows // 8, 8, lanes), -jnp.inf)
        s_s[...] = s3
        m = jnp.max(jnp.max(s3, axis=0), axis=0, keepdims=True)
        m_safe = jnp.where(m > -jnp.inf, m, 0.0)
        w3 = jnp.exp2((s_s[...] - m_safe[None]) * scale2)
        st_ref[pl.ds(g, 1), :] = m
        st_ref[pl.ds(n_groups + g, 1), :] = jnp.sum(jnp.sum(w3, axis=0), axis=0, keepdims=True)
        w_t = w3.reshape(rows, lanes).astype(BF16).T
        mix = jnp.zeros((lanes, D), F32)
        for p in range(GB // 2):
            vals = jnp.concatenate([v_vm[g * GB + 2 * p], v_vm[g * GB + 2 * p + 1]], axis=1)
            o = jnp.dot(w_t, vals, preferred_element_type=F32)
            mix = jnp.where(row_l % GB == 2 * p, o[:, :D], mix)
            mix = jnp.where(row_l % GB == 2 * p + 1, o[:, D:], mix)
        mix_ref[:, pl.ds(pl.multiple_of(g * GB, GB), GB), :] = mix.reshape(heads, GB, D)
        return carry

    lax.fori_loop(0, n_groups, group, 0)
    for g in range(n_groups):
        ko_copy(g).wait()
        vo_copy(g).wait()


def combine_kernel(dims, mix_ref, st_ref, wo_hbm, y_ref,
                   wo_vm, r_mix, r_st, c_t, o_s, p_send, p_recv, y_send, y_recv, y_all,
                   wo_sem, mix_ssem, mix_rsem, st_ssem, st_rsem, p_ssem, p_rsem, y_ssem, y_rsem,
                   a_ssem, a_rsem, f_ssem, f_rsem):
    groups, n_seq, n_head, n_groups, blk = dims
    head_i, seq_i = lax.axis_index("head"), lax.axis_index("seq")
    x_i, core_i = seq_i // 2, seq_i % 2
    n_x = n_seq // 2
    batch = n_groups * GB
    scale2 = (D ** -0.5) * LOG2E

    wo_copy = pltpu.make_async_copy(wo_hbm, wo_vm, wo_sem)
    wo_copy.start()
    barrier = pltpu.get_barrier_semaphore()
    for dh in range(n_head):
        for ds in range(n_seq):
            if dh or ds:
                pl.semaphore_signal(barrier, inc=1, device_id={
                    "head": (head_i + dh) % n_head, "seq": (seq_i + ds) % n_seq}, device_id_type=MESH)
    pl.semaphore_wait(barrier, n_head * n_seq - 1)

    copies = []
    for k in range(1, n_seq):
        to = (seq_i + k) % n_seq
        a = pltpu.make_async_remote_copy(st_ref, r_st.at[k - 1], st_ssem.at[k - 1], st_rsem.at[k - 1],
                                         device_id={"seq": to}, device_id_type=MESH)
        a.start()
        b = pltpu.make_async_remote_copy(mix_ref.at[pl.ds(to * groups, groups)], r_mix.at[k - 1],
                                         mix_ssem.at[k - 1], mix_rsem.at[k - 1],
                                         device_id={"seq": to}, device_id_type=MESH)
        b.start()
        copies.append((a, b))
    for a, b in copies:
        a.wait()
    ms = [st_ref[:n_groups]] + [r_st[k, :n_groups] for k in range(n_seq - 1)]
    ls = [st_ref[n_groups:]] + [r_st[k, n_groups:] for k in range(n_seq - 1)]
    top = functools.reduce(jnp.maximum, ms)
    es = [jnp.exp2((m - top) * scale2) for m in ms]
    total = functools.reduce(jnp.add, [l * e for l, e in zip(ls, es)])
    for k in range(n_seq):
        c_t[k] = (es[k] / total).T
    for a, b in copies:
        b.wait()
    for g in range(groups):
        tiles = []
        at = pl.ds(pl.multiple_of((seq_i * groups + g) * GB, GB), GB)
        cs = [c_t[k, at, :] for k in range(n_seq)]
        for n in range(n_groups):
            o = None
            for k in range(n_seq):
                src = mix_ref[seq_i * groups + g, n * GB:(n + 1) * GB, :] if k == 0 else r_mix[k - 1, g, n * GB:(n + 1) * GB, :]
                term = src * cs[k][:, n:n + 1]
                o = term if o is None else o + term
            tiles.append(o)
        o_s[:, g * D:(g + 1) * D] = jnp.concatenate(tiles, axis=0).astype(BF16)
    wo_copy.wait()

    def block_of(dh, dx, core):
        h, x = (head_i + dh) % n_head, (x_i + dx) % n_x
        return h, x * 2 + core, h * n_seq + x * 2 + core

    def product(b):
        return jnp.dot(o_s[...], wo_vm[:, pl.ds(pl.multiple_of(b * blk, blk), blk)], preferred_element_type=F32)

    order = [(dh, dx) for dh in range(n_head - 1, -1, -1) for dx in range(n_x - 1, -1, -1)]
    partner = {"seq": x_i * 2 + 1 - core_i}
    p_copies, y_copies = {}, {}
    for dh, dx in order:
        i = dh * n_x + dx
        _, _, b = block_of(dh, dx, 1 - core_i)
        p_send[i] = product(b)
        p_copies[i] = pltpu.make_async_remote_copy(p_send.at[i], p_recv.at[i], p_ssem.at[i], p_rsem.at[i],
                                                   device_id=partner, device_id_type=MESH)
        p_copies[i].start()
    own = None
    for dh, dx in order:
        i = dh * n_x + dx
        h, s, b = block_of(dh, dx, core_i)
        part = product(b)
        p_copies[i].wait_recv()
        part = part + p_recv[i]
        if i:
            y_send[i - 1] = part
            y_copies[i] = pltpu.make_async_remote_copy(y_send.at[i - 1], y_recv.at[i - 1], y_ssem.at[i - 1],
                                                       y_rsem.at[i - 1], device_id={"head": h, "seq": s},
                                                       device_id_type=MESH)
            y_copies[i].start()
        else:
            own = part
    for i in sorted(y_copies):
        y_copies[i].wait_recv()
        own = own + y_recv[i - 1]
    mine = head_i * n_seq + seq_i
    y_all[mine] = own.astype(BF16)
    gathers = {}
    for dh, dx in order:
        i = dh * n_x + dx
        h, s, b = block_of(dh, dx, core_i)
        if i:
            gathers[i] = pltpu.make_async_remote_copy(y_all.at[mine], y_all.at[mine], a_ssem.at[i - 1], a_rsem.at[i - 1],
                                                      device_id={"head": h, "seq": s}, device_id_type=MESH)
            gathers[i].start()
    forwards = {}
    for i in range(n_head * n_x):
        dh, dx = i // n_x, i % n_x
        _, _, b = block_of(dh, dx, core_i)
        if i:
            gathers[i].wait_recv()
        forwards[i] = pltpu.make_async_remote_copy(y_all.at[b], y_all.at[b], f_ssem.at[i], f_rsem.at[i],
                                                   device_id=partner, device_id_type=MESH)
        forwards[i].start()
    for i in forwards:
        forwards[i].wait()
    for i in p_copies:
        p_copies[i].wait_send()
    for i in y_copies:
        y_copies[i].wait_send()
        gathers[i].wait_send()
    for b in range(n_head * n_seq):
        y_ref[:, b * blk:(b + 1) * blk] = y_all[b]


def solution(mesh):
    n_head, n_seq = mesh.shape["head"], mesh.shape["seq"]
    cache_spec = P("rep", "seq", "head", None)

    def step(tokens, w_query, w_key, w_value, w_out, k_cache, v_cache, positions):
        batch, shard, kv, d = k_cache.shape
        model = tokens.shape[1]
        heads = w_query.shape[1] // d // n_head
        groups = heads // kv
        n_groups = batch // GB
        rows, lanes = shard * kv, heads * GB
        slots = 3
        any_spec = pl.BlockSpec(memory_space=pl.ANY)
        vmem = pl.BlockSpec(memory_space=pltpu.VMEM)
        flat = (batch, rows, d)
        dma = pltpu.SemaphoreType.DMA
        k_out, v_out, mix, stats = pl.pallas_call(
            functools.partial(attend_kernel, (kv, groups, shard, n_groups, slots)),
            name="attend",
            out_shape=(jax.ShapeDtypeStruct(flat, BF16), jax.ShapeDtypeStruct(flat, BF16),
                       jax.ShapeDtypeStruct((heads, batch, d), F32),
                       jax.ShapeDtypeStruct((2 * n_groups, lanes), F32)),
            in_specs=[pl.BlockSpec(memory_space=pltpu.SMEM), vmem] + [any_spec] * 5,
            out_specs=(any_spec, any_spec, vmem, vmem),
            scratch_shapes=[
                pltpu.VMEM(flat, BF16), pltpu.VMEM(flat, BF16),
                pltpu.VMEM((slots, model, kv * d), BF16),
                pltpu.VMEM((heads, batch, d), F32), pltpu.VMEM((kv, batch, d), F32),
                pltpu.VMEM((kv, batch, d), F32), pltpu.VMEM((rows // 8, 8, lanes), F32),
                dma((slots,)), dma((n_groups,)), dma((n_groups,)), dma((n_groups,)), dma((n_groups,)),
            ],
            compiler_params=pltpu.CompilerParams(vmem_limit_bytes=58 * MIB),
        )(positions, tokens, w_query, w_key, w_value, k_cache.reshape(flat), v_cache.reshape(flat))

        n_dev = n_head * n_seq
        blk = w_out.shape[1] // n_dev
        n_x = n_seq // 2
        chips = n_head * n_x
        y = pl.pallas_call(
            functools.partial(combine_kernel, (groups, n_seq, n_head, n_groups, blk)),
            name="combine",
            out_shape=jax.ShapeDtypeStruct((batch, w_out.shape[1]), BF16),
            in_specs=[vmem, vmem, any_spec],
            out_specs=vmem,
            scratch_shapes=[
                pltpu.VMEM(w_out.shape, BF16),
                pltpu.VMEM((n_seq - 1, groups, batch, d), F32), pltpu.VMEM((n_seq - 1, 2 * n_groups, lanes), F32),
                pltpu.VMEM((n_seq, lanes, n_groups), F32), pltpu.VMEM((batch, groups * d), BF16),
                pltpu.VMEM((chips, batch, blk), F32), pltpu.VMEM((chips, batch, blk), F32),
                pltpu.VMEM((chips - 1, batch, blk), F32), pltpu.VMEM((chips - 1, batch, blk), F32),
                pltpu.VMEM((n_dev, batch, blk), BF16),
                dma, dma((n_seq - 1,)), dma((n_seq - 1,)), dma((n_seq - 1,)), dma((n_seq - 1,)),
                dma((chips,)), dma((chips,)), dma((chips - 1,)), dma((chips - 1,)),
                dma((chips - 1,)), dma((chips - 1,)), dma((chips,)), dma((chips,)),
            ],
            compiler_params=pltpu.CompilerParams(collective_id=0, has_side_effects=True, vmem_limit_bytes=32 * MIB),
        )(mix, stats, w_out)
        return y, k_out.reshape(k_cache.shape), v_out.reshape(v_cache.shape)

    return jax.shard_map(
        step,
        mesh=mesh,
        in_specs=(P("rep", None), P(), P(), P(), P(("head", "seq"), None), cache_spec, cache_spec, P("rep")),
        out_specs=(P("rep", None), cache_spec, cache_spec),
        check_vma=False,
    )
```

time: 158 us -> 62.4 us (0.39)
  blocking collectives: 61.8 us -> 0 us
  Pallas kernels: 0 us -> 59.1 us
  matrix products: 37 us -> 0 us
  other arithmetic: 28.3 us -> 0 us
  waiting for transfers between devices: 14.9 us -> 0 us
  between operations: 14.2 us -> 0.67 us
    pallas_call x0 -> x2, Pallas kernels: none -> 59.1 us  [the longest x1 31.8 us: step(): pl.pallas_call(functools.partial(attend_kernel, (kv, groups, shard, n_gro...]
    psum x2 -> x0, blocking collectives: 47 us -> none  [the longest x1 33.1 us: local_step(): y_total = lax.psum(y_part, ('head', 'seq'))]
    dot_general x6 -> x0, matrix products: 37 us -> none  [the longest x1 10.4 us: local_step(): jnp.einsum('bkgd,btkd->bkgt', query, k_new, preferred_element_type=jnp.fl...]
    select_n x2 -> x0, other arithmetic: 25.9 us -> none  [the longest x1 25.9 us: local_step(): k_new = jnp.where(is_slot, new_key, k_cache)]
    psum x1 -> x0, waiting for transfers between devices: 14.9 us -> none  [local_step(): lax.psum((local_sum * rescale, local_mix * rescale[..., None]), 'seq')]
    pmax x1 -> x0, blocking collectives: 14.8 us -> none  [local_step(): global_max = lax.pmax(local_max, 'seq')]
  transfers between devices with their start and end apart: 1 -> 0, of which waited for: 1 -> 0; matrix products, arithmetic and copies ran while one was open for 0% -> 0% of each run, Pallas kernels for 0% -> 0%
where the time goes in v1:
time: 62.4 us; the launch traced here: 62.3 us
  Pallas kernels  59.1 us (95%)
  local copies, waits for them, and re-layouts  2.53 us (4%)
  between operations  0.67 us (1%)
    pallas_call x1, Pallas kernels, step(): pl.pallas_call(functools.partial(attend_kernel, (kv, groups, shard, n_gro...  31.8 us
    pallas_call x1, Pallas kernels, step(): pl.pallas_call(functools.partial(combine_kernel, (groups, n_seq, n_head,...  27.3 us
    unnamed x7, local copies, waits for them, and re-layouts  2.53 us

profile of v1, /device:TPU:0, one launch (start us, length us, event | category | flops | bytes accessed | tf_op | source)
XLA Modules:
  0.0 62.3 jit_solution(935143758352024091)
XLA Ops:
  0.6 0.0 copy-start
  0.6 31.8 %attend.1 = (bf16[64,1024,128]{2,1,0:T(8,128)(2,1)}, bf16[64,1024,128]{2,1,0:T(8,128)(2,1)}, f32[16,64,128]{2,1,0:T(8,128)}, f32[16,128]{1,0:T(8,128)}) custom-call(s32[64]{0:T(128)} %pos_ref.1, bf16[64,4096]{1,0:T(8,128)(2,1)} %x_ref.1, bf16[4096,4096]{1,0:T(8,128)(2,1)} %wq.1, bf16[4096,1024]{1,0:T(8,128)(2,1)} %wk.1, bf16[4096,1024]{1,0:T(8,128)(2,1)} %wv.1, ...), custom_call_target="tpu_custom_call" | custom-call | tf_op jit(solution)/shard_map/attend/pallas_call | solution.py:290
  32.5 0.0 copy-done
  32.5 0.0 copy-start.1
  32.5 1.0 %copy-done.1 = f32[16,64,128]{2,1,0:T(8,128)S(1)} copy-done((f32[16,64,128]{2,1,0:T(8,128)S(1)}, f32[16,64,128]{2,1,0:T(8,128)}, u32[]{:S(2)}) %copy-start.1) | copy-done | bytes 524312
  33.5 0.0 copy-start.2
  33.5 0.7 %copy-done.2 = f32[16,128]{1,0:T(8,128)S(1)} copy-done((f32[16,128]{1,0:T(8,128)S(1)}, f32[16,128]{1,0:T(8,128)}, u32[]{:S(2)}) %copy-start.2) | copy-done | bytes 8216
  34.2 27.3 %combine.1 = bf16[64,4096]{1,0:T(8,128)(2,1)S(1)} custom-call(f32[16,64,128]{2,1,0:T(8,128)S(1)} %copy-done.1, f32[16,128]{1,0:T(8,128)S(1)} %copy-done.2, bf16[512,4096]{1,0:T(8,128)(2,1)S(1)} %copy-done), custom_call_target="tpu_custom_call" | custom-call | tf_op jit(solution)/shard_map/combine/pallas_call | solution.py:312
  61.5 0.8 %copy.12 = bf16[64,4096]{1,0:T(8,128)(2,1)} copy(bf16[64,4096]{1,0:T(8,128)(2,1)S(1)} %combine.1) | data formatting | bytes 1048576
Async XLA Ops:
  0.6 31.8 %copy-start = (bf16[512,4096]{1,0:T(8,128)(2,1)S(1)}, bf16[512,4096]{1,0:T(8,128)(2,1)}, u32[]{:S(2)}) copy-start(bf16[512,4096]{1,0:T(8,128)(2,1)} %wo_hbm.1) | copy-start | bytes 12582916
  32.5 1.0 %copy-start.1 = (f32[16,64,128]{2,1,0:T(8,128)S(1)}, f32[16,64,128]{2,1,0:T(8,128)}, u32[]{:S(2)}) copy-start(f32[16,64,128]{2,1,0:T(8,128)} %get-tuple-element.7.mix_ref) | copy-start | bytes 1572868
  33.5 0.7 %copy-start.2 = (f32[16,128]{1,0:T(8,128)S(1)}, f32[16,128]{1,0:T(8,128)}, u32[]{:S(2)}) copy-start(f32[16,128]{1,0:T(8,128)} %get-tuple-element.8.st_ref) | copy-start | bytes 24580

commit v2 on v0

v2 whole, which is shorter than its diff:
```python
import functools

import jax
import jax.numpy as jnp
from jax import lax
from jax.experimental import pallas as pl
from jax.experimental.pallas import tpu as pltpu
from jax.sharding import PartitionSpec as P

MESH = pl.DeviceIdType.MESH
BF16 = jnp.bfloat16
F32 = jnp.float32
MIB = 2 ** 20
GB = 8
D = 128
LOG2E = 1.4426950408889634
SCALE2 = (D ** -0.5) * LOG2E
CHUNKS = ((0, 4), (4, 4))


def step_kernel(dims, pos_hbm, x_hbm, wq, wk, wv, wo_hbm, kc, vc, new_s, kv_vm, y_ref,
                pos_ref, x_vm, w_vm, wo_vm, q_s, s_s, wt_s, mix_s, st_s, r_mix, r_st, m_t, l_t, o_s,
                p_send, p_recv, y_send, y_recv, y_all,
                in_sem, w_sem, k_sem, v_sem, mix_ssem, mix_rsem, st_ssem, st_rsem,
                p_ssem, p_rsem, y_ssem, y_rsem, a_ssem, a_rsem, f_ssem, f_rsem):
    kv, groups, shard, n_groups, slots, n_seq, n_head, blk = dims
    heads = kv * groups
    rows = shard * kv
    lanes = heads * GB
    head_i, seq_i = lax.axis_index("head"), lax.axis_index("seq")
    x_i, core_i = seq_i // 2, seq_i % 2
    n_x = n_seq // 2
    base = seq_i * shard
    cols = kv * D
    n_q = heads // kv
    k_vm, v_vm, nk_s, nv_s = kv_vm.at[0], kv_vm.at[1], new_s.at[0], new_s.at[1]

    barrier = pltpu.get_barrier_semaphore()
    for dh in range(n_head):
        for ds in range(n_seq):
            if dh or ds:
                pl.semaphore_signal(barrier, inc=1, device_id={
                    "head": (head_i + dh) % n_head, "seq": (seq_i + ds) % n_seq}, device_id_type=MESH)

    def w_copy(c):
        if c < n_q:
            src, at = wq, head_i * (heads * D) + c * cols
        else:
            src, at = (wk, wv)[c - n_q], head_i * cols
        at = pl.multiple_of(at, cols)
        return pltpu.make_async_copy(src.at[:, pl.ds(at, cols)], w_vm.at[c % slots], w_sem.at[c % slots])

    def k_copy(g):
        at = pl.ds(g * GB, GB)
        return pltpu.make_async_copy(kc.at[at], k_vm.at[at], k_sem.at[g])

    def v_copy(g):
        at = pl.ds(g * GB, GB)
        return pltpu.make_async_copy(vc.at[at], v_vm.at[at], v_sem.at[g])

    x_copy = pltpu.make_async_copy(x_hbm, x_vm, in_sem.at[0])
    pos_copy = pltpu.make_async_copy(pos_hbm, pos_ref, in_sem.at[1])
    wo_copy = pltpu.make_async_copy(wo_hbm, wo_vm, in_sem.at[2])
    x_copy.start()
    pos_copy.start()

    n_w = n_q + 2
    ahead = 4
    for c in range(min(slots, n_w)):
        w_copy(c).start()
    issued = 0
    x_copy.wait()
    for c in range(n_w):
        w_copy(c).wait()
        r = jnp.dot(x_vm[...], w_vm[c % slots], preferred_element_type=F32)
        r = r.astype(BF16).astype(F32)
        for i in range(kv):
            part = r[:, i * D:(i + 1) * D]
            if c < n_q:
                q_s[c * kv + i] = part
            elif c == n_q:
                nk_s[i] = part
            else:
                nv_s[i] = part
        if c + slots < n_w:
            w_copy(c + slots).start()
        else:
            while issued < min(ahead, n_groups) and issued <= (c + slots - n_w + 1):
                k_copy(issued).start()
                v_copy(issued).start()
                issued += 1
    for g in range(issued, min(ahead, n_groups)):
        k_copy(g).start()
        v_copy(g).start()
    pos_copy.wait()

    sub = lax.broadcasted_iota(jnp.int32, (8, lanes), 0)
    lane = lax.broadcasted_iota(jnp.int32, (8, lanes), 1)
    lane_d = lax.broadcasted_iota(jnp.int32, (D, lanes), 1)
    row_l = lax.broadcasted_iota(jnp.int32, (lanes, D), 0)
    per_tile = 8 // kv
    half = rows // 2

    def rows_of(g):
        return pl.ds(pl.multiple_of(g * GB, GB), GB)

    def scores(g):
        q_t = q_s[:, rows_of(g), :].reshape(lanes, D).T
        accs = [None, None]
        for p in range(GB // 2):
            qs = jnp.concatenate([jnp.where(lane_d % GB == 2 * p, q_t, 0.0),
                                  jnp.where(lane_d % GB == 2 * p + 1, q_t, 0.0)], axis=0).astype(BF16)
            for h in range(2):
                at = pl.ds(h * half, half)
                keys = jnp.concatenate([k_vm[g * GB + 2 * p, at, :], k_vm[g * GB + 2 * p + 1, at, :]], axis=1)
                s = jnp.dot(keys, qs, preferred_element_type=F32)
                accs[h] = s if accs[h] is None else accs[h] + s
        for h in range(2):
            s_s[pl.ds(h * (half // 8), half // 8)] = accs[h].reshape(half // 8, 8, lanes)

    def softmax(g):
        pos_row = jnp.zeros((8, lanes), jnp.int32)
        for i in range(GB):
            pos_row = jnp.where(lane % GB == i, pos_ref[g * GB + i] - base, pos_row)
        limit = jnp.where(sub % kv == lane // (groups * GB), pos_row - 1 - sub // kv, -1)
        tile_t = lax.broadcasted_iota(jnp.int32, (rows // 8, 8, lanes), 0) * per_tile
        s3 = jnp.where(limit[None] >= tile_t, s_s[...], -jnp.inf)
        m = jnp.max(jnp.max(s3, axis=0), axis=0, keepdims=True)
        m_safe = jnp.where(m > -jnp.inf, m, 0.0)
        w3 = jnp.exp2((s3 - m_safe[None]) * SCALE2)
        total = jnp.sum(jnp.sum(w3, axis=0), axis=0, keepdims=True)
        st_s[g] = jnp.where(sub == 0, m, total)
        wt_s[...] = w3.reshape(rows, lanes).astype(BF16).T

    def values(g):
        mix = jnp.zeros((lanes, D), F32)
        for p in range(GB // 2):
            vals = jnp.concatenate([v_vm[g * GB + 2 * p], v_vm[g * GB + 2 * p + 1]], axis=1)
            o = jnp.dot(wt_s[...], vals, preferred_element_type=F32)
            mix = jnp.where(row_l % GB == 2 * p, o[:, :D], mix)
            mix = jnp.where(row_l % GB == 2 * p + 1, o[:, D:], mix)
        mix_s[:, rows_of(g), :] = mix.reshape(heads, GB, D)

    def mix_copy(g, k):
        to = (seq_i + k) % n_seq
        return pltpu.make_async_remote_copy(
            mix_s.at[pl.ds(to * groups, groups), rows_of(g)], r_mix.at[k - 1, :, rows_of(g)],
            mix_ssem.at[g, k - 1], mix_rsem.at[g, k - 1], device_id={"seq": to}, device_id_type=MESH)

    def st_copy(g, k):
        to = (seq_i + k) % n_seq
        return pltpu.make_async_remote_copy(st_s.at[g], r_st.at[k - 1, g], st_ssem.at[g, k - 1], st_rsem.at[g, k - 1],
                                            device_id={"seq": to}, device_id_type=MESH)

    order = [(dh, dx) for dh in range(n_head - 1, -1, -1) for dx in range(n_x - 1, -1, -1)]
    partner = {"seq": x_i * 2 + 1 - core_i}
    mine = head_i * n_seq + seq_i

    def block_of(dh, dx, core):
        h, x = (head_i + dh) % n_head, (x_i + dx) % n_x
        return h, x * 2 + core, h * n_seq + x * 2 + core

    def p_copy(c, i):
        at = pl.ds(CHUNKS[c][0] * GB, CHUNKS[c][1] * GB)
        return pltpu.make_async_remote_copy(p_send.at[i, at], p_recv.at[i, at], p_ssem.at[c, i], p_rsem.at[c, i],
                                            device_id=partner, device_id_type=MESH)

    def y_copy(c, dh, dx):
        i = dh * n_x + dx
        at = pl.ds(CHUNKS[c][0] * GB, CHUNKS[c][1] * GB)
        h, s, _ = block_of(dh, dx, core_i)
        return pltpu.make_async_remote_copy(y_send.at[i, at], y_recv.at[i - 1, at], y_ssem.at[c, i - 1],
                                            y_rsem.at[c, i - 1], device_id={"head": h, "seq": s}, device_id_type=MESH)

    def a_copy(c, dh, dx):
        i = dh * n_x + dx
        at = pl.ds(CHUNKS[c][0] * GB, CHUNKS[c][1] * GB)
        h, s, _ = block_of(dh, dx, core_i)
        return pltpu.make_async_remote_copy(y_all.at[mine, at], y_all.at[mine, at], a_ssem.at[c, i - 1],
                                            a_rsem.at[c, i - 1], device_id={"head": h, "seq": s}, device_id_type=MESH)

    def f_copy(c, dh, dx):
        i = dh * n_x + dx
        at = pl.ds(CHUNKS[c][0] * GB, CHUNKS[c][1] * GB)
        _, _, b = block_of(dh, dx, core_i)
        return pltpu.make_async_remote_copy(y_all.at[b, at], y_all.at[b, at], f_ssem.at[c, i], f_rsem.at[c, i],
                                            device_id=partner, device_id_type=MESH)

    def out_products(c):
        g0, n = CHUNKS[c]
        for g in range(g0, g0 + n):
            for k in range(1, n_seq):
                st_copy(g, k).wait()
        own_rows = pl.ds(pl.multiple_of(seq_i * groups * GB, groups * GB), groups * GB)
        for k in range(n_seq):
            src = st_s if k == 0 else r_st.at[k - 1]
            m_t[k] = jnp.concatenate([src[g, 0:1, :] for g in range(g0, g0 + n)], axis=0).T
            l_t[k] = jnp.concatenate([src[g, 1:2, :] for g in range(g0, g0 + n)], axis=0).T
        ms = [m_t[k, own_rows, :] for k in range(n_seq)]
        ls = [l_t[k, own_rows, :] for k in range(n_seq)]
        col = lax.broadcasted_iota(jnp.int32, (GB, n), 1)
        fresh = []
        for j in range(groups):
            s_new = jnp.zeros((GB, n), F32)
            for t in range(n):
                at = pl.ds((g0 + t) * GB, GB)
                dot = jnp.sum(q_s[seq_i * groups + j, at, :] * nk_s[seq_i, at, :], axis=1, keepdims=True)
                s_new = jnp.where(col == t, dot, s_new)
            fresh.append(s_new)
        m_new = jnp.concatenate(fresh, axis=0)
        top = functools.reduce(jnp.maximum, ms + [m_new])
        es = [jnp.exp2((m - top) * SCALE2) for m in ms]
        e_new = jnp.exp2((m_new - top) * SCALE2)
        total = functools.reduce(jnp.add, [l * e for l, e in zip(ls, es)] + [e_new])
        cs = [e / total for e in es]
        c_new = e_new / total
        for g in range(g0, g0 + n):
            for k in range(1, n_seq):
                mix_copy(g, k).wait()
        for j in range(groups):
            tiles = []
            for t in range(n):
                at = pl.ds((g0 + t) * GB, GB)
                o = nv_s[seq_i, at, :] * c_new[j * GB:(j + 1) * GB, t:t + 1]
                for k in range(n_seq):
                    src = mix_s[seq_i * groups + j, at, :] if k == 0 else r_mix[k - 1, j, at, :]
                    o = o + src * cs[k][j * GB:(j + 1) * GB, t:t + 1]
                tiles.append(o)
            o_s[pl.ds(g0 * GB, n * GB), j * D:(j + 1) * D] = jnp.concatenate(tiles, axis=0).astype(BF16)
        at = pl.ds(g0 * GB, n * GB)
        o = o_s[at, :]

        def product(b):
            return jnp.dot(o, wo_vm[:, pl.ds(pl.multiple_of(b * blk, blk), blk)], preferred_element_type=F32)

        for dh, dx in order:
            i = dh * n_x + dx
            p_send[i, at, :] = product(block_of(dh, dx, 1 - core_i)[2])
            p_copy(c, i).start()
        for dh, dx in order:
            y_send[dh * n_x + dx, at, :] = product(block_of(dh, dx, core_i)[2])

    def out_scatter(c):
        at = pl.ds(CHUNKS[c][0] * GB, CHUNKS[c][1] * GB)
        for dh, dx in order:
            i = dh * n_x + dx
            p_copy(c, i).wait_recv()
            y_send[i, at, :] = y_send[i, at, :] + p_recv[i, at, :]
            if i:
                y_copy(c, dh, dx).start()

    def out_gather(c):
        at = pl.ds(CHUNKS[c][0] * GB, CHUNKS[c][1] * GB)
        own = y_send[0, at, :]
        for dh, dx in reversed(order[:-1]):
            y_copy(c, dh, dx).wait_recv()
            own = own + y_recv[dh * n_x + dx - 1, at, :]
        y_all[mine, at, :] = own.astype(BF16)
        for dh, dx in order[:-1]:
            a_copy(c, dh, dx).start()
        f_copy(c, 0, 0).start()

    def out_forward(c):
        for dh, dx in reversed(order[:-1]):
            a_copy(c, dh, dx).wait_recv()
            f_copy(c, dh, dx).start()

    def out_finish(c):
        for dh, dx in order:
            f_copy(c, dh, dx).wait()
            p_copy(c, dh * n_x + dx).wait_send()
            if dh or dx:
                y_copy(c, dh, dx).wait_send()
                a_copy(c, dh, dx).wait_send()

    k_copy(0).wait()
    scores(0)
    softmax(0)
    pl.semaphore_wait(barrier, n_head * n_seq - 1)
    wo_copy.start()

    def group(g, carry):
        @pl.when(g + ahead < n_groups)
        def _():
            k_copy(g + ahead).start()
            v_copy(g + ahead).start()
        v_copy(g).wait()
        k_copy(g + 1).wait()
        scores(g + 1)
        values(g)
        for k in range(1, n_seq):
            st_copy(g, k).start()
            mix_copy(g, k).start()
        softmax(g + 1)

        @pl.when(g == 4)
        def _():
            wo_copy.wait()
            out_products(0)

        @pl.when(g == 5)
        def _():
            out_scatter(0)

        return carry

    lax.fori_loop(0, n_groups - 1, group, 0)
    last = n_groups - 1
    v_copy(last).wait()
    values(last)
    for k in range(1, n_seq):
        st_copy(last, k).start()
        mix_copy(last, k).start()
    out_gather(0)
    out_products(1)
    out_scatter(1)
    out_forward(0)
    out_gather(1)
    out_forward(1)
    out_finish(0)
    out_finish(1)
    for b in range(n_head * n_seq):
        y_ref[:, b * blk:(b + 1) * blk] = y_all[b]


def write_kernel(dims, pos_ref, new, kv_new, ko, vo, patch, o_sem, p_sem):
    shard, n_groups = dims
    batch = n_groups * GB
    base = lax.axis_index("seq") * shard
    outs = (ko, vo)

    def copy(side, g):
        at = pl.ds(g * GB, GB)
        return pltpu.make_async_copy(kv_new.at[side, at], outs[side].at[at], o_sem.at[side, g])

    def patch_copy(side, b, t):
        return pltpu.make_async_copy(patch.at[side, b], outs[side].at[b, t], p_sem.at[side, b])

    def place(b):
        t = pos_ref[b] - base
        return t, jnp.logical_and(t >= 0, t < shard)

    for side in range(2):
        for g in range(n_groups):
            copy(side, g).start()

    def patch_rows(b, carry):
        for side in range(2):
            patch[side, b] = new[side, :, b, :].astype(BF16)
        return carry

    lax.fori_loop(0, batch, patch_rows, 0)
    for side in range(2):
        for g in range(n_groups):
            copy(side, g).wait()
            for i in range(GB):
                b = g * GB + i
                t, hit = place(b)

                @pl.when(hit)
                def _():
                    patch_copy(side, b, t).start()

    def finish(b, carry):
        t, hit = place(b)

        @pl.when(hit)
        def _():
            patch_copy(0, b, t).wait()
            patch_copy(1, b, t).wait()
        return carry

    lax.fori_loop(0, batch, finish, 0)


def solution(mesh):
    n_head, n_seq = mesh.shape["head"], mesh.shape["seq"]
    cache_spec = P("rep", "seq", "head", None)

    def step(tokens, w_query, w_key, w_value, w_out, k_cache, v_cache, positions):
        batch, shard, kv, d = k_cache.shape
        model = tokens.shape[1]
        heads = w_query.shape[1] // d // n_head
        groups = heads // kv
        n_groups = batch // GB
        rows, lanes = shard * kv, heads * GB
        slots = 3
        n_dev = n_head * n_seq
        blk = w_out.shape[1] // n_dev
        chips = n_head * (n_seq // 2)
        n_c = len(CHUNKS)
        c_groups = CHUNKS[0][1]
        hbm = pl.BlockSpec(memory_space=pltpu.HBM)
        any_spec = pl.BlockSpec(memory_space=pl.ANY)
        vmem = pl.BlockSpec(memory_space=pltpu.VMEM)
        flat = (batch, rows, d)
        dma = pltpu.SemaphoreType.DMA
        fresh, kv_raw, y = pl.pallas_call(
            functools.partial(step_kernel, (kv, groups, shard, n_groups, slots, n_seq, n_head, blk)),
            name="step",
            out_shape=(pltpu.VMEM((2, kv, batch, d), F32), pltpu.VMEM((2, *flat), BF16),
                       jax.ShapeDtypeStruct((batch, w_out.shape[1]), BF16)),
            in_specs=[hbm] * 8,
            out_specs=(vmem,) * 3,
            scratch_shapes=[
                pltpu.SMEM((batch,), jnp.int32), pltpu.VMEM((batch, model), BF16),
                pltpu.VMEM((slots, model, kv * d), BF16), pltpu.VMEM(w_out.shape, BF16),
                pltpu.VMEM((heads, batch, d), F32), pltpu.VMEM((rows // 8, 8, lanes), F32),
                pltpu.VMEM((lanes, rows), BF16), pltpu.VMEM((heads, batch, d), F32),
                pltpu.VMEM((n_groups, 8, lanes), F32),
                pltpu.VMEM((n_seq - 1, groups, batch, d), F32), pltpu.VMEM((n_seq - 1, n_groups, 8, lanes), F32),
                pltpu.VMEM((n_seq, lanes, c_groups), F32), pltpu.VMEM((n_seq, lanes, c_groups), F32),
                pltpu.VMEM((batch, groups * d), BF16),
                pltpu.VMEM((chips, batch, blk), F32), pltpu.VMEM((chips, batch, blk), F32),
                pltpu.VMEM((chips, batch, blk), F32), pltpu.VMEM((chips - 1, batch, blk), F32),
                pltpu.VMEM((n_dev, batch, blk), BF16),
                dma((3,)), dma((slots,)), dma((n_groups,)), dma((n_groups,)),
                dma((n_groups, n_seq - 1)), dma((n_groups, n_seq - 1)),
                dma((n_groups, n_seq - 1)), dma((n_groups, n_seq - 1)),
                dma((n_c, chips)), dma((n_c, chips)), dma((n_c, chips - 1)), dma((n_c, chips - 1)),
                dma((n_c, chips - 1)), dma((n_c, chips - 1)), dma((n_c, chips)), dma((n_c, chips)),
            ],
            compiler_params=pltpu.CompilerParams(collective_id=0, has_side_effects=True, vmem_limit_bytes=28 * MIB),
        )(positions, tokens, w_query, w_key, w_value, w_out, k_cache.reshape(flat), v_cache.reshape(flat))

        k_out, v_out = pl.pallas_call(
            functools.partial(write_kernel, (shard, n_groups)), name="write",
            out_shape=(jax.ShapeDtypeStruct(k_cache.shape, BF16), jax.ShapeDtypeStruct(k_cache.shape, BF16)),
            in_specs=[pl.BlockSpec(memory_space=pltpu.SMEM), vmem, any_spec],
            out_specs=(any_spec, any_spec),
            scratch_shapes=[pltpu.VMEM((2, batch, kv, d), BF16), dma((2, n_groups)), dma((2, batch))],
            compiler_params=pltpu.CompilerParams(vmem_limit_bytes=4 * MIB),
        )(positions, fresh, kv_raw.reshape(2, *k_cache.shape))
        return y, k_out, v_out

    return jax.shard_map(
        step,
        mesh=mesh,
        in_specs=(P("rep", None), P(), P(), P(), P(("head", "seq"), None), cache_spec, cache_spec, P("rep")),
        out_specs=(P("rep", None), cache_spec, cache_spec),
        check_vma=False,
    )
```

time: 158 us -> 60 us (0.38)
  blocking collectives: 61.8 us -> 0 us
  Pallas kernels: 0 us -> 58.4 us
  matrix products: 37 us -> 0 us
  other arithmetic: 28.3 us -> 0 us
  waiting for transfers between devices: 14.9 us -> 0 us
  between operations: 14.2 us -> 0.68 us
    pallas_call x0 -> x2, Pallas kernels: none -> 58.4 us  [the longest x1 45.1 us: step(): pl.pallas_call(functools.partial(step_kernel, (kv, groups, shard, n_group...]
    psum x2 -> x0, blocking collectives: 47 us -> none  [the longest x1 33.1 us: local_step(): y_total = lax.psum(y_part, ('head', 'seq'))]
    dot_general x6 -> x0, matrix products: 37 us -> none  [the longest x1 10.4 us: local_step(): jnp.einsum('bkgd,btkd->bkgt', query, k_new, preferred_element_type=jnp.fl...]
    select_n x2 -> x0, other arithmetic: 25.9 us -> none  [the longest x1 25.9 us: local_step(): k_new = jnp.where(is_slot, new_key, k_cache)]
    psum x1 -> x0, waiting for transfers between devices: 14.9 us -> none  [local_step(): lax.psum((local_sum * rescale, local_mix * rescale[..., None]), 'seq')]
    pmax x1 -> x0, blocking collectives: 14.8 us -> none  [local_step(): global_max = lax.pmax(local_max, 'seq')]
  transfers between devices with their start and end apart: 1 -> 0, of which waited for: 1 -> 0; matrix products, arithmetic and copies ran while one was open for 0% -> 0% of each run, Pallas kernels for 0% -> 0%
where the time goes in v2:
time: 60 us; the launch traced here: 59.9 us
  Pallas kernels  58.4 us (97%)
  local copies, waits for them, and re-layouts  0.8 us (1%)
  between operations  0.68 us (1%)
    pallas_call x1, Pallas kernels, step(): pl.pallas_call(functools.partial(step_kernel, (kv, groups, shard, n_group...  45.1 us
    pallas_call x1, Pallas kernels, step(): pl.pallas_call(functools.partial(write_kernel, (shard, n_groups)), name='...  13.3 us

profile of v2, /device:TPU:0, one launch (start us, length us, event | category | flops | bytes accessed | tf_op | source)
XLA Modules:
  0.0 59.9 jit_solution(14295612746964570148)
XLA Ops:
  0.6 0.0 copy-start
  0.6 45.1 %step.1 = (f32[2,4,64,128]{3,2,1,0:T(8,128)S(1)}, bf16[2,64,1024,128]{3,2,1,0:T(8,128)(2,1)S(1)}, bf16[64,4096]{1,0:T(8,128)(2,1)}) custom-call(s32[64]{0:T(128)} %pos_ref.1, bf16[64,4096]{1,0:T(8,128)(2,1)} %x_hbm.1, bf16[4096,4096]{1,0:T(8,128)(2,1)} %wq.1, bf16[4096,1024]{1,0:T(8,128)(2,1)} %wk.1, bf16[4096,1024]{1,0:T(8,128)(2,1)} %wv.1, ...), custom_call_target="tpu_custom_call" | custom-call | tf_op jit(solution)/shard_map/step/pallas_call | solution.py:398
  45.7 0.0 copy-done
  45.7 0.0 copy-start.1
  45.8 13.3 %write.1 = (bf16[64,256,4,128]{3,2,1,0:T(4,128)(2,1)}, bf16[64,256,4,128]{3,2,1,0:T(4,128)(2,1)}) custom-call(s32[64]{0:T(128)S(1)} %copy-done, f32[2,4,64,128]{3,2,1,0:T(8,128)S(1)} %get-tuple-element.9.new, bf16[2,64,256,4,128]{4,3,2,1,0:T(4,128)(2,1)S(1)} %bitcast.3), custom_call_target="tpu_custom_call" | custom-call | tf_op jit(solution)/shard_map/write/pallas_call | solution.py:426
  59.1 0.0 copy-done.1
  59.1 0.8 %copy.12 = bf16[64,4096]{1,0:T(8,128)(2,1)} copy(bf16[64,4096]{1,0:T(8,128)(2,1)S(1)} %copy-done.1) | data formatting | bytes 1048576
Async XLA Ops:
  0.6 45.1 %copy-start = (s32[64]{0:T(128)S(1)}, s32[64]{0:T(128)}, u32[]{:S(2)}) copy-start(s32[64]{0:T(128)} %pos_ref.1) | copy-start | bytes 772
  45.7 13.3 %copy-start.1 = (bf16[64,4096]{1,0:T(8,128)(2,1)S(1)}, bf16[64,4096]{1,0:T(8,128)(2,1)}, u32[]{:S(2)}) copy-start(bf16[64,4096]{1,0:T(8,128)(2,1)} %get-tuple-element.16) | copy-start | bytes 1572868

commit v3 on v2

--- a/solution.py
+++ b/solution.py
@@ -18,10 +18,10 @@
 CHUNKS = ((0, 4), (4, 4))
 
 
-def step_kernel(dims, pos_hbm, x_hbm, wq, wk, wv, wo_hbm, kc, vc, new_s, kv_vm, y_ref,
+def step_kernel(dims, pos_hbm, x_hbm, wq, wk, wv, wo_hbm, kc, vc, new_s, y_ref, kv_vm,
                 pos_ref, x_vm, w_vm, wo_vm, q_s, s_s, wt_s, mix_s, st_s, r_mix, r_st, m_t, l_t, o_s,
                 p_send, p_recv, y_send, y_recv, y_all,
-                in_sem, w_sem, k_sem, v_sem, mix_ssem, mix_rsem, st_ssem, st_rsem,
+                in_sem, w_sem, k_sem, v_sem, h_ssem, h_rsem, mix_ssem, mix_rsem, st_ssem, st_rsem,
                 p_ssem, p_rsem, y_ssem, y_rsem, a_ssem, a_rsem, f_ssem, f_rsem):
     kv, groups, shard, n_groups, slots, n_seq, n_head, blk = dims
     heads = kv * groups
@@ -33,6 +33,7 @@
     base = seq_i * shard
     cols = kv * D
     n_q = heads // kv
+    partner = {"seq": x_i * 2 + 1 - core_i}
     k_vm, v_vm, nk_s, nv_s = kv_vm.at[0], kv_vm.at[1], new_s.at[0], new_s.at[1]
 
     barrier = pltpu.get_barrier_semaphore()
@@ -42,13 +43,16 @@
                 pl.semaphore_signal(barrier, inc=1, device_id={
                     "head": (head_i + dh) % n_head, "seq": (seq_i + ds) % n_seq}, device_id_type=MESH)
 
-    def w_copy(c):
-        if c < n_q:
-            src, at = wq, head_i * (heads * D) + c * cols
-        else:
-            src, at = (wk, wv)[c - n_q], head_i * cols
-        at = pl.multiple_of(at, cols)
-        return pltpu.make_async_copy(src.at[:, pl.ds(at, cols)], w_vm.at[c % slots], w_sem.at[c % slots])
+    half_cols = cols // 2
+    q_mine = n_q // 2
+
+    def w_copies(c):
+        if c < q_mine:
+            at = pl.multiple_of(head_i * (heads * D) + (core_i * q_mine + c) * cols, cols)
+            return [pltpu.make_async_copy(wq.at[:, pl.ds(at, cols)], w_vm.at[c], w_sem.at[c])]
+        at = pl.multiple_of(head_i * cols + core_i * half_cols, half_cols)
+        return [pltpu.make_async_copy(src.at[:, pl.ds(at, half_cols)], w_vm.at[c, :, pl.ds(n * half_cols, half_cols)],
+                                      w_sem.at[c + n]) for n, src in enumerate((wk, wv))]
 
     def k_copy(g):
         at = pl.ds(g * GB, GB)
@@ -64,40 +68,47 @@
     x_copy.start()
     pos_copy.start()
 
-    n_w = n_q + 2
     ahead = 4
-    for c in range(min(slots, n_w)):
-        w_copy(c).start()
-    issued = 0
+    for c in range(q_mine + 1):
+        for copy in w_copies(c):
+            copy.start()
     x_copy.wait()
-    for c in range(n_w):
-        w_copy(c).wait()
-        r = jnp.dot(x_vm[...], w_vm[c % slots], preferred_element_type=F32)
+    hq = heads // 2
+    q_part = q_s.at[:, pl.ds(pl.multiple_of(core_i * hq, hq), hq)]
+    n_part = new_s.at[:, pl.ds(core_i * (kv // 2), kv // 2)]
+    q_share = pltpu.make_async_remote_copy(q_part, q_part, h_ssem.at[0], h_rsem.at[0],
+                                           device_id=partner, device_id_type=MESH)
+    n_share = pltpu.make_async_remote_copy(n_part, n_part, h_ssem.at[1], h_rsem.at[1],
+                                           device_id=partner, device_id_type=MESH)
+    for c in range(q_mine + 1):
+        for copy in w_copies(c):
+            copy.wait()
+        if c < ahead:
+            k_copy(c).start()
+            v_copy(c).start()
+        r = jnp.dot(x_vm[...], w_vm[c], preferred_element_type=F32)
         r = r.astype(BF16).astype(F32)
-        for i in range(kv):
-            part = r[:, i * D:(i + 1) * D]
-            if c < n_q:
-                q_s[c * kv + i] = part
-            elif c == n_q:
-                nk_s[i] = part
-            else:
-                nv_s[i] = part
-        if c + slots < n_w:
-            w_copy(c + slots).start()
+        if c < q_mine:
+            for i in range(kv):
+                q_s[:, core_i * hq + c * kv + i, :] = r[:, i * D:(i + 1) * D]
         else:
-            while issued < min(ahead, n_groups) and issued <= (c + slots - n_w + 1):
-                k_copy(issued).start()
-                v_copy(issued).start()
-                issued += 1
-    for g in range(issued, min(ahead, n_groups)):
+            for n in range(2):
+                for i in range(kv // 2):
+                    new_s[n, core_i * (kv // 2) + i] = r[:, n * half_cols + i * D:n * half_cols + (i + 1) * D]
+        if c == q_mine - 1:
+            pl.semaphore_wait(barrier, n_head * n_seq - 1)
+            q_share.start()
+    n_share.start()
+    for g in range(q_mine + 1, ahead):
         k_copy(g).start()
         v_copy(g).start()
+    q_share.wait()
+    n_share.wait()
     pos_copy.wait()
 
     sub = lax.broadcasted_iota(jnp.int32, (8, lanes), 0)
     lane = lax.broadcasted_iota(jnp.int32, (8, lanes), 1)
     lane_d = lax.broadcasted_iota(jnp.int32, (D, lanes), 1)
-    row_l = lax.broadcasted_iota(jnp.int32, (lanes, D), 0)
     per_tile = 8 // kv
     half = rows // 2
 
@@ -105,11 +116,11 @@
         return pl.ds(pl.multiple_of(g * GB, GB), GB)
 
     def scores(g):
-        q_t = q_s[:, rows_of(g), :].reshape(lanes, D).T
+        q_t = q_s[rows_of(g)].reshape(lanes, D).T
         accs = [None, None]
         for p in range(GB // 2):
-            qs = jnp.concatenate([jnp.where(lane_d % GB == 2 * p, q_t, 0.0),
-                                  jnp.where(lane_d % GB == 2 * p + 1, q_t, 0.0)], axis=0).astype(BF16)
+            qs = jnp.concatenate([jnp.where(lane_d // heads == 2 * p, q_t, 0.0),
+                                  jnp.where(lane_d // heads == 2 * p + 1, q_t, 0.0)], axis=0).astype(BF16)
             for h in range(2):
                 at = pl.ds(h * half, half)
                 keys = jnp.concatenate([k_vm[g * GB + 2 * p, at, :], k_vm[g * GB + 2 * p + 1, at, :]], axis=1)
@@ -121,8 +132,8 @@
     def softmax(g):
         pos_row = jnp.zeros((8, lanes), jnp.int32)
         for i in range(GB):
-            pos_row = jnp.where(lane % GB == i, pos_ref[g * GB + i] - base, pos_row)
-        limit = jnp.where(sub % kv == lane // (groups * GB), pos_row - 1 - sub // kv, -1)
+            pos_row = jnp.where(lane // heads == i, pos_ref[g * GB + i] - base, pos_row)
+        limit = jnp.where(sub % kv == lane % heads // groups, pos_row - 1 - sub // kv, -1)
         tile_t = lax.broadcasted_iota(jnp.int32, (rows // 8, 8, lanes), 0) * per_tile
         s3 = jnp.where(limit[None] >= tile_t, s_s[...], -jnp.inf)
         m = jnp.max(jnp.max(s3, axis=0), axis=0, keepdims=True)
@@ -133,13 +144,9 @@
         wt_s[...] = w3.reshape(rows, lanes).astype(BF16).T
 
     def values(g):
-        mix = jnp.zeros((lanes, D), F32)
-        for p in range(GB // 2):
-            vals = jnp.concatenate([v_vm[g * GB + 2 * p], v_vm[g * GB + 2 * p + 1]], axis=1)
-            o = jnp.dot(wt_s[...], vals, preferred_element_type=F32)
-            mix = jnp.where(row_l % GB == 2 * p, o[:, :D], mix)
-            mix = jnp.where(row_l % GB == 2 * p + 1, o[:, D:], mix)
-        mix_s[:, rows_of(g), :] = mix.reshape(heads, GB, D)
+        for i in range(GB):
+            b = g * GB + i
+            mix_s[:, b, :] = jnp.dot(wt_s[i * heads:(i + 1) * heads, :], v_vm[b], preferred_element_type=F32)
 
     def mix_copy(g, k):
         to = (seq_i + k) % n_seq
@@ -153,7 +160,6 @@
                                             device_id={"seq": to}, device_id_type=MESH)
 
     order = [(dh, dx) for dh in range(n_head - 1, -1, -1) for dx in range(n_x - 1, -1, -1)]
-    partner = {"seq": x_i * 2 + 1 - core_i}
     mine = head_i * n_seq + seq_i
 
     def block_of(dh, dx, core):
@@ -191,20 +197,23 @@
         for g in range(g0, g0 + n):
             for k in range(1, n_seq):
                 st_copy(g, k).wait()
-        own_rows = pl.ds(pl.multiple_of(seq_i * groups * GB, groups * GB), groups * GB)
         for k in range(n_seq):
             src = st_s if k == 0 else r_st.at[k - 1]
             m_t[k] = jnp.concatenate([src[g, 0:1, :] for g in range(g0, g0 + n)], axis=0).T
             l_t[k] = jnp.concatenate([src[g, 1:2, :] for g in range(g0, g0 + n)], axis=0).T
-        ms = [m_t[k, own_rows, :] for k in range(n_seq)]
-        ls = [l_t[k, own_rows, :] for k in range(n_seq)]
+
+        def own(ref, k):
+            return jnp.concatenate([ref[k, pl.ds(seq_i * groups + j, GB, stride=heads), :] for j in range(groups)], axis=0)
+
+        ms = [own(m_t, k) for k in range(n_seq)]
+        ls = [own(l_t, k) for k in range(n_seq)]
         col = lax.broadcasted_iota(jnp.int32, (GB, n), 1)
         fresh = []
         for j in range(groups):
             s_new = jnp.zeros((GB, n), F32)
             for t in range(n):
                 at = pl.ds((g0 + t) * GB, GB)
-                dot = jnp.sum(q_s[seq_i * groups + j, at, :] * nk_s[seq_i, at, :], axis=1, keepdims=True)
+                dot = jnp.sum(q_s[at, seq_i * groups + j, :] * nk_s[seq_i, at, :], axis=1, keepdims=True)
                 s_new = jnp.where(col == t, dot, s_new)
             fresh.append(s_new)
         m_new = jnp.concatenate(fresh, axis=0)
@@ -276,7 +285,6 @@
     k_copy(0).wait()
     scores(0)
     softmax(0)
-    pl.semaphore_wait(barrier, n_head * n_seq - 1)
     wo_copy.start()
 
     def group(g, carry):
@@ -323,54 +331,29 @@
         y_ref[:, b * blk:(b + 1) * blk] = y_all[b]
 
 
-def write_kernel(dims, pos_ref, new, kv_new, ko, vo, patch, o_sem, p_sem):
+def write_kernel(dims, pos_ref, new, y_in, kv_in, ko, vo, y_out, kv_vm, o_sem, y_sem):
     shard, n_groups = dims
-    batch = n_groups * GB
+    del kv_in
     base = lax.axis_index("seq") * shard
     outs = (ko, vo)
-
-    def copy(side, g):
+    copies = [pltpu.make_async_copy(y_in, y_out, y_sem)]
+    copies[0].start()
+    for g in range(n_groups):
+        for i in range(GB):
+            b = g * GB + i
+            t = pos_ref[b] - base
+
+            @pl.when(jnp.logical_and(t >= 0, t < shard))
+            def _():
+                for side in range(2):
+                    kv_vm[side, b, t] = new[side, :, b, :].astype(BF16)
+
         at = pl.ds(g * GB, GB)
-        return pltpu.make_async_copy(kv_new.at[side, at], outs[side].at[at], o_sem.at[side, g])
-
-    def patch_copy(side, b, t):
-        return pltpu.make_async_copy(patch.at[side, b], outs[side].at[b, t], p_sem.at[side, b])
-
-    def place(b):
-        t = pos_ref[b] - base
-        return t, jnp.logical_and(t >= 0, t < shard)
-
-    for side in range(2):
-        for g in range(n_groups):
-            copy(side, g).start()
-
-    def patch_rows(b, carry):
         for side in range(2):
-            patch[side, b] = new[side, :, b, :].astype(BF16)
-        return carry
-
-    lax.fori_loop(0, batch, patch_rows, 0)
-    for side in range(2):
-        for g in range(n_groups):
-            copy(side, g).wait()
-            for i in range(GB):
-                b = g * GB + i
-                t, hit = place(b)
-
-                @pl.when(hit)
-                def _():
-                    patch_copy(side, b, t).start()
-
-    def finish(b, carry):
-        t, hit = place(b)
-
-        @pl.when(hit)
-        def _():
-            patch_copy(0, b, t).wait()
-            patch_copy(1, b, t).wait()
-        return carry
-
-    lax.fori_loop(0, batch, finish, 0)
+            copies.append(pltpu.make_async_copy(kv_vm.at[side, at], outs[side].at[at], o_sem.at[side, g]))
+            copies[-1].start()
+    for c in copies:
+        c.wait()
 
 
 def solution(mesh):
@@ -384,7 +367,7 @@
         groups = heads // kv
         n_groups = batch // GB
         rows, lanes = shard * kv, heads * GB
-        slots = 3
+        slots = heads // kv // 2 + 1
         n_dev = n_head * n_seq
         blk = w_out.shape[1] // n_dev
         chips = n_head * (n_seq // 2)
@@ -395,17 +378,17 @@
         vmem = pl.BlockSpec(memory_space=pltpu.VMEM)
         flat = (batch, rows, d)
         dma = pltpu.SemaphoreType.DMA
-        fresh, kv_raw, y = pl.pallas_call(
+        fresh, y, kv_raw = pl.pallas_call(
             functools.partial(step_kernel, (kv, groups, shard, n_groups, slots, n_seq, n_head, blk)),
             name="step",
-            out_shape=(pltpu.VMEM((2, kv, batch, d), F32), pltpu.VMEM((2, *flat), BF16),
-                       jax.ShapeDtypeStruct((batch, w_out.shape[1]), BF16)),
+            out_shape=(pltpu.VMEM((2, kv, batch, d), F32), pltpu.VMEM((batch, w_out.shape[1]), BF16),
+                       pltpu.VMEM((2, *flat), BF16)),
             in_specs=[hbm] * 8,
             out_specs=(vmem,) * 3,
             scratch_shapes=[
                 pltpu.SMEM((batch,), jnp.int32), pltpu.VMEM((batch, model), BF16),
                 pltpu.VMEM((slots, model, kv * d), BF16), pltpu.VMEM(w_out.shape, BF16),
-                pltpu.VMEM((heads, batch, d), F32), pltpu.VMEM((rows // 8, 8, lanes), F32),
+                pltpu.VMEM((batch, heads, d), F32), pltpu.VMEM((rows // 8, 8, lanes), F32),
                 pltpu.VMEM((lanes, rows), BF16), pltpu.VMEM((heads, batch, d), F32),
                 pltpu.VMEM((n_groups, 8, lanes), F32),
                 pltpu.VMEM((n_seq - 1, groups, batch, d), F32), pltpu.VMEM((n_seq - 1, n_groups, 8, lanes), F32),
@@ -414,7 +397,7 @@
                 pltpu.VMEM((chips, batch, blk), F32), pltpu.VMEM((chips, batch, blk), F32),
                 pltpu.VMEM((chips, batch, blk), F32), pltpu.VMEM((chips - 1, batch, blk), F32),
                 pltpu.VMEM((n_dev, batch, blk), BF16),
-                dma((3,)), dma((slots,)), dma((n_groups,)), dma((n_groups,)),
+                dma((3,)), dma((slots + 1,)), dma((n_groups,)), dma((n_groups,)), dma((2,)), dma((2,)),
                 dma((n_groups, n_seq - 1)), dma((n_groups, n_seq - 1)),
                 dma((n_groups, n_seq - 1)), dma((n_groups, n_seq - 1)),
                 dma((n_c, chips)), dma((n_c, chips)), dma((n_c, chips - 1)), dma((n_c, chips - 1)),
@@ -423,15 +406,17 @@
             compiler_params=pltpu.CompilerParams(collective_id=0, has_side_effects=True, vmem_limit_bytes=28 * MIB),
         )(positions, tokens, w_query, w_key, w_value, w_out, k_cache.reshape(flat), v_cache.reshape(flat))
 
-        k_out, v_out = pl.pallas_call(
+        k_out, v_out, y_out, _ = pl.pallas_call(
             functools.partial(write_kernel, (shard, n_groups)), name="write",
-            out_shape=(jax.ShapeDtypeStruct(k_cache.shape, BF16), jax.ShapeDtypeStruct(k_cache.shape, BF16)),
-            in_specs=[pl.BlockSpec(memory_space=pltpu.SMEM), vmem, any_spec],
-            out_specs=(any_spec, any_spec),
-            scratch_shapes=[pltpu.VMEM((2, batch, kv, d), BF16), dma((2, n_groups)), dma((2, batch))],
+            out_shape=(jax.ShapeDtypeStruct(k_cache.shape, BF16), jax.ShapeDtypeStruct(k_cache.shape, BF16),
+                       jax.ShapeDtypeStruct(y.shape, BF16), pltpu.VMEM((2, *k_cache.shape), BF16)),
+            in_specs=[pl.BlockSpec(memory_space=pltpu.SMEM), vmem, any_spec, vmem],
+            out_specs=(any_spec, any_spec, any_spec, vmem),
+            scratch_shapes=[dma((2, n_groups)), dma],
+            input_output_aliases={3: 3},
             compiler_params=pltpu.CompilerParams(vmem_limit_bytes=4 * MIB),
-        )(positions, fresh, kv_raw.reshape(2, *k_cache.shape))
-        return y, k_out, v_out
+        )(positions, fresh, y, kv_raw.reshape(2, *k_cache.shape))
+        return y_out, k_out, v_out
 
     return jax.shard_map(
         step,

time: 60 us -> 54 us (0.900)
  Pallas kernels: 58.4 us -> 53.3 us
  local copies, waits for them, and re-layouts: 0.8 us -> 0.01 us
    pallas_call x1, Pallas kernels: 45.1 us -> 41.5 us  [step(): pl.pallas_call(functools.partial(step_kernel, (kv, groups, shard, n_group...]
    pallas_call x1, Pallas kernels: 13.3 us -> 11.8 us  [step(): pl.pallas_call(functools.partial(write_kernel, (shard, n_groups)), name='...]
    unnamed x5 -> x2, local copies, waits for them, and re-layouts: 0.8 us -> 0.01 us
where the time goes in v3:
time: 54 us; the launch traced here: 53.9 us
  Pallas kernels  53.3 us (99%)
  between operations  0.66 us (1%)
    pallas_call x1, Pallas kernels, step(): pl.pallas_call(functools.partial(step_kernel, (kv, groups, shard, n_group...  41.5 us
    pallas_call x1, Pallas kernels, step(): pl.pallas_call(functools.partial(write_kernel, (shard, n_groups)), name='...  11.8 us

profile of v3, /device:TPU:0, one launch (start us, length us, event | category | flops | bytes accessed | tf_op | source)
XLA Modules:
  0.0 53.9 jit_solution(6056452127725827572)
XLA Ops:
  0.6 0.0 copy-start
  0.6 41.5 %step.1 = (f32[2,4,64,128]{3,2,1,0:T(8,128)S(1)}, bf16[64,4096]{1,0:T(8,128)(2,1)S(1)}, bf16[2,64,1024,128]{3,2,1,0:T(8,128)(2,1)S(1)}) custom-call(s32[64]{0:T(128)} %pos_ref.1, bf16[64,4096]{1,0:T(8,128)(2,1)} %x_hbm.1, bf16[4096,4096]{1,0:T(8,128)(2,1)} %wq.1, bf16[4096,1024]{1,0:T(8,128)(2,1)} %wk.1, bf16[4096,1024]{1,0:T(8,128)(2,1)} %wv.1, ...), custom_call_target="tpu_custom_call" | custom-call | tf_op jit(solution)/shard_map/step/pallas_call | solution.py:381
  42.2 0.0 copy-done
  42.2 11.8 %write.1 = (bf16[64,256,4,128]{3,2,1,0:T(4,128)(2,1)}, bf16[64,256,4,128]{3,2,1,0:T(4,128)(2,1)}, bf16[64,4096]{1,0:T(8,128)(2,1)}, bf16[2,64,256,4,128]{4,3,2,1,0:T(4,128)(2,1)S(1)}) custom-call(s32[64]{0:T(128)S(1)} %copy-done, f32[2,4,64,128]{3,2,1,0:T(8,128)S(1)} %get-tuple-element.9.new, ...), custom_call_target="tpu_custom_call", output_to_operand_aliasing={{3}: (3, {})} | custom-call | tf_op jit(solution)/shard_map/write/pallas_call | solution.py:409
Async XLA Ops:
  0.6 41.5 %copy-start = (s32[64]{0:T(128)S(1)}, s32[64]{0:T(128)}, u32[]{:S(2)}) copy-start(s32[64]{0:T(128)} %pos_ref.1) | copy-start | bytes 772

commit v4 on v3

--- a/solution.py
+++ b/solution.py
@@ -15,11 +15,11 @@
 D = 128
 LOG2E = 1.4426950408889634
 SCALE2 = (D ** -0.5) * LOG2E
-CHUNKS = ((0, 4), (4, 4))
+CHUNKS = ((0, 6), (6, 2))
 
 
 def step_kernel(dims, pos_hbm, x_hbm, wq, wk, wv, wo_hbm, kc, vc, new_s, y_ref, kv_vm,
-                pos_ref, x_vm, w_vm, wo_vm, q_s, s_s, wt_s, mix_s, st_s, r_mix, r_st, m_t, l_t, o_s,
+                pos_ref, x_vm, w_vm, wo_vm, q_s, qt_s, s_s, wt_s, mix_s, st_s, r_mix, r_st, m_t, l_t, o_s,
                 p_send, p_recv, y_send, y_recv, y_all,
                 in_sem, w_sem, k_sem, v_sem, h_ssem, h_rsem, mix_ssem, mix_rsem, st_ssem, st_rsem,
                 p_ssem, p_rsem, y_ssem, y_rsem, a_ssem, a_rsem, f_ssem, f_rsem):
@@ -113,10 +113,10 @@
     half = rows // 2
 
     def rows_of(g):
-        return pl.ds(pl.multiple_of(g * GB, GB), GB)
+        return pl.ds(g * GB if isinstance(g, int) else pl.multiple_of(g * GB, GB), GB)
 
     def scores(g):
-        q_t = q_s[rows_of(g)].reshape(lanes, D).T
+        q_t = qt_s[g]
         accs = [None, None]
         for p in range(GB // 2):
             qs = jnp.concatenate([jnp.where(lane_d // heads == 2 * p, q_t, 0.0),
@@ -141,12 +141,12 @@
         w3 = jnp.exp2((s3 - m_safe[None]) * SCALE2)
         total = jnp.sum(jnp.sum(w3, axis=0), axis=0, keepdims=True)
         st_s[g] = jnp.where(sub == 0, m, total)
-        wt_s[...] = w3.reshape(rows, lanes).astype(BF16).T
+        wt_s[g % 2] = w3.reshape(rows, lanes).astype(BF16).T
 
     def values(g):
         for i in range(GB):
             b = g * GB + i
-            mix_s[:, b, :] = jnp.dot(wt_s[i * heads:(i + 1) * heads, :], v_vm[b], preferred_element_type=F32)
+            mix_s[:, b, :] = jnp.dot(wt_s[g % 2, i * heads:(i + 1) * heads, :], v_vm[b], preferred_element_type=F32)
 
     def mix_copy(g, k):
         to = (seq_i + k) % n_seq
@@ -199,11 +199,11 @@
                 st_copy(g, k).wait()
         for k in range(n_seq):
             src = st_s if k == 0 else r_st.at[k - 1]
-            m_t[k] = jnp.concatenate([src[g, 0:1, :] for g in range(g0, g0 + n)], axis=0).T
-            l_t[k] = jnp.concatenate([src[g, 1:2, :] for g in range(g0, g0 + n)], axis=0).T
+            m_t[k, :, 0:n] = jnp.concatenate([src[g, 0:1, :] for g in range(g0, g0 + n)], axis=0).T
+            l_t[k, :, 0:n] = jnp.concatenate([src[g, 1:2, :] for g in range(g0, g0 + n)], axis=0).T
 
         def own(ref, k):
-            return jnp.concatenate([ref[k, pl.ds(seq_i * groups + j, GB, stride=heads), :] for j in range(groups)], axis=0)
+            return jnp.concatenate([ref[k, pl.ds(seq_i * groups + j, GB, stride=heads), 0:n] for j in range(groups)], axis=0)
 
         ms = [own(m_t, k) for k in range(n_seq)]
         ls = [own(l_t, k) for k in range(n_seq)]
@@ -282,6 +282,8 @@
                 y_copy(c, dh, dx).wait_send()
                 a_copy(c, dh, dx).wait_send()
 
+    for g in range(n_groups):
+        qt_s[g] = q_s[rows_of(g)].reshape(lanes, D).T
     k_copy(0).wait()
     scores(0)
     softmax(0)
@@ -296,20 +298,10 @@
         k_copy(g + 1).wait()
         scores(g + 1)
         values(g)
+        softmax(g + 1)
         for k in range(1, n_seq):
             st_copy(g, k).start()
             mix_copy(g, k).start()
-        softmax(g + 1)
-
-        @pl.when(g == 4)
-        def _():
-            wo_copy.wait()
-            out_products(0)
-
-        @pl.when(g == 5)
-        def _():
-            out_scatter(0)
-
         return carry
 
     lax.fori_loop(0, n_groups - 1, group, 0)
@@ -319,9 +311,12 @@
     for k in range(1, n_seq):
         st_copy(last, k).start()
         mix_copy(last, k).start()
-    out_gather(0)
+    wo_copy.wait()
+    out_products(0)
+    out_scatter(0)
     out_products(1)
     out_scatter(1)
+    out_gather(0)
     out_forward(0)
     out_gather(1)
     out_forward(1)
@@ -372,7 +367,7 @@
         blk = w_out.shape[1] // n_dev
         chips = n_head * (n_seq // 2)
         n_c = len(CHUNKS)
-        c_groups = CHUNKS[0][1]
+        c_groups = max(n for _, n in CHUNKS)
         hbm = pl.BlockSpec(memory_space=pltpu.HBM)
         any_spec = pl.BlockSpec(memory_space=pl.ANY)
         vmem = pl.BlockSpec(memory_space=pltpu.VMEM)
@@ -388,8 +383,8 @@
             scratch_shapes=[
                 pltpu.SMEM((batch,), jnp.int32), pltpu.VMEM((batch, model), BF16),
                 pltpu.VMEM((slots, model, kv * d), BF16), pltpu.VMEM(w_out.shape, BF16),
-                pltpu.VMEM((batch, heads, d), F32), pltpu.VMEM((rows // 8, 8, lanes), F32),
-                pltpu.VMEM((lanes, rows), BF16), pltpu.VMEM((heads, batch, d), F32),
+                pltpu.VMEM((batch, heads, d), F32), pltpu.VMEM((n_groups, d, lanes), F32), pltpu.VMEM((rows // 8, 8, lanes), F32),
+                pltpu.VMEM((2, lanes, rows), BF16), pltpu.VMEM((heads, batch, d), F32),
                 pltpu.VMEM((n_groups, 8, lanes), F32),
                 pltpu.VMEM((n_seq - 1, groups, batch, d), F32), pltpu.VMEM((n_seq - 1, n_groups, 8, lanes), F32),
                 pltpu.VMEM((n_seq, lanes, c_groups), F32), pltpu.VMEM((n_seq, lanes, c_groups), F32),

time: 54 us -> 51.1 us (0.946)
  Pallas kernels: 53.3 us -> 50.3 us
    pallas_call x1, Pallas kernels: 41.5 us -> 38.5 us  [step(): pl.pallas_call(functools.partial(step_kernel, (kv, groups, shard, n_group...]
where the time goes in v4:
time: 51.1 us; the launch traced here: 51 us
  Pallas kernels  50.3 us (98%)
  between operations  0.66 us (1%)
    pallas_call x1, Pallas kernels, step(): pl.pallas_call(functools.partial(step_kernel, (kv, groups, shard, n_group...  38.5 us
    pallas_call x1, Pallas kernels, step(): pl.pallas_call(functools.partial(write_kernel, (shard, n_groups)), name='...  11.8 us

profile of v4, /device:TPU:0, one launch (start us, length us, event | category | flops | bytes accessed | tf_op | source)
XLA Modules:
  0.0 51.0 jit_solution(1979100476175282579)
XLA Ops:
  0.6 0.0 copy-start
  0.6 38.5 %step.1 = (f32[2,4,64,128]{3,2,1,0:T(8,128)S(1)}, bf16[64,4096]{1,0:T(8,128)(2,1)S(1)}, bf16[2,64,1024,128]{3,2,1,0:T(8,128)(2,1)S(1)}) custom-call(s32[64]{0:T(128)} %pos_ref.1, bf16[64,4096]{1,0:T(8,128)(2,1)} %x_hbm.1, bf16[4096,4096]{1,0:T(8,128)(2,1)} %wq.1, bf16[4096,1024]{1,0:T(8,128)(2,1)} %wk.1, bf16[4096,1024]{1,0:T(8,128)(2,1)} %wv.1, ...), custom_call_target="tpu_custom_call" | custom-call | tf_op jit(solution)/shard_map/step/pallas_call | solution.py:376
  39.2 0.0 copy-done
  39.2 11.8 %write.1 = (bf16[64,256,4,128]{3,2,1,0:T(4,128)(2,1)}, bf16[64,256,4,128]{3,2,1,0:T(4,128)(2,1)}, bf16[64,4096]{1,0:T(8,128)(2,1)}, bf16[2,64,256,4,128]{4,3,2,1,0:T(4,128)(2,1)S(1)}) custom-call(s32[64]{0:T(128)S(1)} %copy-done, f32[2,4,64,128]{3,2,1,0:T(8,128)S(1)} %get-tuple-element.9.new, ...), custom_call_target="tpu_custom_call", output_to_operand_aliasing={{3}: (3, {})} | custom-call | tf_op jit(solution)/shard_map/write/pallas_call | solution.py:404
Async XLA Ops:
  0.6 38.6 %copy-start = (s32[64]{0:T(128)S(1)}, s32[64]{0:T(128)}, u32[]{:S(2)}) copy-start(s32[64]{0:T(128)} %pos_ref.1) | copy-start | bytes 772
